TPU v7x, 32 devices: a whole 2x2x4 slice. The times are simulated.
32 devices in a mesh: dp: 4 (over x, core), fsdp: 4 (over z), mp: 2 (over y).
Axes of the slice: x: 2, y: 2, z: 4, core: 2. Of those that a mesh axis runs over, the one named last changes fastest.
Arguments:
- tokens_in: bfloat16 [4096, 3072], P(('dp', 'fsdp', 'mp')), may hold values from -40 to 40
- segment_ids: int32 [4096], P(('dp', 'fsdp', 'mp')), may hold values from 0 to 31, never falling along the last dimension, each value on 1 to 512 neighbouring positions
- target_ids: int32 [4096], P(('dp', 'fsdp', 'mp')), may hold values from 0 to 8191
- old_weights: bfloat16 [4, 3072, 2048], P(None, ('dp', 'fsdp', 'mp'))
- old_first: float32 [4, 3072, 2048], P(None, ('dp', 'fsdp', 'mp')), may hold values from -6 to 6
- old_second: float32 [4, 3072, 2048], P(None, ('dp', 'fsdp', 'mp')), may hold values from 0.01 to 4
- old_block: int32 [32], P(('dp', 'fsdp', 'mp')), may hold values from 0 to 31, each once
- new_residue: int32 [4], P('dp'), may hold values from 0 to 3, each once
- norm_gain: float32 [3072], replicated, may hold values from 0.5 to 1.5
- head_weight: bfloat16 [3072, 8192], P(None, ('fsdp', 'mp'))
Outputs:
- new_weights: bfloat16 [4, 3072, 2048], P(None, 'dp', ('fsdp', 'mp'))
- new_first: float32 [4, 3072, 2048], P(None, 'dp', ('fsdp', 'mp'))
- new_second: float32 [4, 3072, 2048], P(None, 'dp', ('fsdp', 'mp'))
- loss: float32 [4096], P(('dp', 'fsdp', 'mp'))
Inputs may be any that keep to these rules, and one draw needn't show every extreme that they name: `old_block`: a permutation of the old layout's row blocks. `new_residue`: a permutation; index i of dp holds the rows whose number modulo 4 is new_residue[i], in rising order. `segment_ids`: never falling along the tokens.
All inputs are finite; a program needn't handle non-finite values.
Results may differ from a plain program's by a relative error of at most 0.0075.
Values may be sent and summed in bfloat16 or wider, within the bound.
A program may use at most 192 MiB of HBM per device.

v0:
```python
import math
import jax
import jax.numpy as jnp
from jax import lax
from jax.sharding import PartitionSpec as P

HD = 128


def inverse_of(table):
    total_count = table.shape[0]
    places = jnp.arange(total_count, dtype=jnp.int32)
    return jnp.sum(jnp.where(table[None, :] == places[:, None], places[None, :], 0), axis=1)


def pack_rows(stored, residues, fm_count):
    matrices, row_count, columns = stored.shape
    dp_count = residues.shape[0]
    split_rows = stored.reshape(
        matrices, row_count // dp_count, dp_count, fm_count, columns // fm_count
    )
    chosen = jnp.take(split_rows, residues, axis=2, mode="clip")
    return chosen.transpose(2, 3, 0, 1, 4).reshape(
        dp_count * fm_count, matrices, row_count // dp_count, columns // fm_count
    )


def unpack_rows(received, holder):
    ordered = jnp.take(received, holder, axis=0, mode="clip")
    devices, matrices, pair_rows, group_cols = ordered.shape
    return ordered.transpose(1, 0, 2, 3).reshape(matrices, devices * pair_rows, group_cols)


def norm_rows(hidden, norm_gain):
    scale = lax.rsqrt(jnp.mean(hidden * hidden, axis=1, keepdims=True) + 1e-05)
    return (hidden * scale * norm_gain).astype(jnp.bfloat16)


FLAGS = dict(tail="a2a", first="before_rs", second="free", tokens="first")


def share_tables(segment_ids, target_ids, old_block, new_residue):
    axes = ("dp", "fsdp", "mp")
    own = jnp.concatenate([segment_ids, target_ids, old_block, new_residue])
    rows = jnp.broadcast_to(own[None, None], (lax.axis_size(axes), 1, own.shape[0]))
    rows = lax.all_to_all(rows, axes, split_axis=0, concat_axis=0, tiled=True)[:, 0]
    count = segment_ids.shape[0]
    fm_count = lax.axis_size(("fsdp", "mp"))
    here = lax.dynamic_slice_in_dim(rows, lax.axis_index("dp") * fm_count, fm_count)
    segments = here[:, :count].reshape(-1)
    targets = here[:, count : 2 * count].reshape(-1)
    return (segments, targets, rows[:, 2 * count], rows[::fm_count, 2 * count + 1])


def joint_loss(row_top, row_total, picked):
    axes = ("fsdp", "mp")
    fm_count = lax.axis_size(axes)
    parts = jnp.stack([row_top, row_total, picked])
    own_count = parts.shape[1] // fm_count
    if FLAGS["tail"] == "a2a":
        parts = parts.reshape(3, fm_count, own_count).transpose(1, 0, 2)
        parts = lax.all_to_all(parts, axes, split_axis=0, concat_axis=0, tiled=True)
    else:
        place = lax.axis_index(axes)
        rows = jnp.zeros((fm_count,) + parts.shape, jnp.float32)
        rows = lax.psum(lax.dynamic_update_slice(rows, parts[None], (place, 0, 0)), axes)
        parts = lax.dynamic_slice_in_dim(rows, place * own_count, own_count, axis=2)
    tops, totals, targets = (parts[:, 0], parts[:, 1], parts[:, 2])
    joint_max = jnp.max(tops, axis=0)
    joint_total = jnp.sum(totals * jnp.exp(tops - joint_max[None]), axis=0)
    return joint_max + jnp.log(joint_total) - jnp.sum(targets, axis=0)


def body(
    tokens_in,
    segment_ids,
    target_ids,
    old_weights,
    old_first,
    old_second,
    old_block,
    new_residue,
    norm_gain,
    head_weight,
):
    dp_count = lax.axis_size("dp")
    fm_count = lax.axis_size(("fsdp", "mp"))
    everyone = ("dp", "fsdp", "mp")
    columns = old_weights.shape[2]
    group_cols = columns // fm_count
    model_width = tokens_in.shape[1]
    new_rows = model_width // dp_count
    segments, targets, table_all, residues = share_tables(
        segment_ids, target_ids, old_block, new_residue
    )
    holder = inverse_of(table_all)
    inverse_res = inverse_of(residues)
    feature_ids = (
        residues[:, None] + dp_count * jnp.arange(new_rows, dtype=jnp.int32)[None]
    ).reshape(-1)
    logical_ids = (
        jnp.arange(new_rows, dtype=jnp.int32)[:, None] + new_rows * inverse_res[None]
    ).reshape(-1)
    own_picked = jnp.take(tokens_in, feature_ids, axis=1, mode="clip")
    picked_cols = lax.all_gather(own_picked, ("fsdp", "mp"), axis=0, tiled=True)
    seq_len = picked_cols.shape[0]
    weights_sent = pack_rows(old_weights, residues, fm_count)
    weights_got = lax.all_to_all(weights_sent, everyone, split_axis=0, concat_axis=0, tiled=True)
    first_sent = pack_rows(old_first, residues, fm_count)
    second_sent = pack_rows(old_second, residues, fm_count)
    if FLAGS["first"] != "free":
        weights_got, first_sent, second_sent = lax.optimization_barrier(
            (weights_got, first_sent, second_sent)
        )
    new_weights = unpack_rows(weights_got, holder)
    projections = new_weights[:3]
    if FLAGS.get("tokens") == "first":
        picked_cols, projections, first_sent = lax.optimization_barrier(
            (picked_cols, projections, first_sent)
        )
    first_got = lax.all_to_all(first_sent, everyone, split_axis=0, concat_axis=0, tiled=True)
    piece = lax.all_gather(projections, "dp", axis=1, tiled=True)
    projected = jnp.einsum("sr,mrc->msc", picked_cols, piece, preferred_element_type=jnp.float32)
    heads = group_cols // HD
    queries = projected[0].astype(jnp.bfloat16).reshape(seq_len, heads, HD)
    keys_all = projected[1].astype(jnp.bfloat16).reshape(seq_len, heads, HD)
    values_all = projected[2].astype(jnp.bfloat16).reshape(seq_len, heads, HD)
    positions_all = jnp.arange(seq_len, dtype=jnp.int32)
    allowed = (positions_all[:, None] >= positions_all[None, :]) & (
        segments[:, None] == segments[None, :]
    )
    scores = jnp.einsum("shd,thd->hst", queries, keys_all, preferred_element_type=jnp.float32) * (
        1.0 / math.sqrt(HD)
    )
    scores = jnp.where(allowed[None], scores, -1e30)
    row_max = jnp.max(scores, axis=2, keepdims=True)
    expo = jnp.where(allowed[None], jnp.exp(scores - row_max), 0.0)
    soft = (expo / jnp.sum(expo, axis=2, keepdims=True)).astype(jnp.bfloat16)
    attended = jnp.einsum("hst,thd->shd", soft, values_all, preferred_element_type=jnp.float32)
    attended = attended.astype(jnp.bfloat16).reshape(seq_len, group_cols)
    shuffled = jnp.einsum(
        "sc,rc->sr",
        attended,
        lax.all_gather(new_weights[3], "dp", axis=0, tiled=True),
        preferred_element_type=jnp.float32,
    )
    partial_value = shuffled.astype(jnp.bfloat16)
    if FLAGS["first"] == "rs_first":
        partial_value, second_sent = lax.optimization_barrier((partial_value, second_sent))
    if FLAGS["first"] == "before_rs":
        partial_value, first_got, second_sent = lax.optimization_barrier(
            (partial_value, first_got, second_sent)
        )
    second_got = lax.all_to_all(second_sent, everyone, split_axis=0, concat_axis=0, tiled=True)
    own_sum = lax.psum_scatter(partial_value, ("fsdp", "mp"), scatter_dimension=0, tiled=True)
    own_sum = jnp.take(own_sum, logical_ids, axis=1, mode="clip").astype(jnp.float32)
    own_normed = norm_rows(tokens_in.astype(jnp.float32) + own_sum, norm_gain)
    if FLAGS["second"] == "before_ag":
        own_normed, second_got = lax.optimization_barrier((own_normed, second_got))
    new_first = unpack_rows(first_got, holder)
    new_second = unpack_rows(second_got, holder)
    normed = lax.all_gather(own_normed, ("fsdp", "mp"), axis=0, tiled=True)
    logits = jnp.dot(normed, head_weight, preferred_element_type=jnp.float32)
    vocab_dev = logits.shape[1]
    offset = lax.axis_index(("fsdp", "mp")) * vocab_dev
    row_top = jnp.max(logits, axis=1)
    row_total = jnp.sum(jnp.exp(logits - row_top[:, None]), axis=1)
    vocab_ids = jnp.arange(vocab_dev, dtype=jnp.int32) + offset
    picked = jnp.sum(jnp.where(vocab_ids[None, :] == targets[:, None], logits, 0.0), axis=1)
    loss = joint_loss(row_top, row_total, picked)
    return (new_weights, new_first, new_second, loss)


def solution(mesh):
    placed = (
        P(("dp", "fsdp", "mp"), None),
        P(("dp", "fsdp", "mp")),
        P(("dp", "fsdp", "mp")),
        P(None, ("dp", "fsdp", "mp"), None),
        P(None, ("dp", "fsdp", "mp"), None),
        P(None, ("dp", "fsdp", "mp"), None),
        P(("dp", "fsdp", "mp")),
        P("dp"),
        P(),
        P(None, ("fsdp", "mp")),
    )
    return jax.shard_map(
        body,
        mesh=mesh,
        in_specs=placed,
        out_specs=(
            P(None, "dp", ("fsdp", "mp")),
            P(None, "dp", ("fsdp", "mp")),
            P(None, "dp", ("fsdp", "mp")),
            P(("dp", "fsdp", "mp")),
        ),
        check_vma=False,
    )
```

profile of v0, /device:TPU:0, one launch (start us, length us, event | category | flops | bytes accessed | tf_op | source)
XLA Modules:
  0.0 589.0 jit_solution(5896758327097351042)
XLA Ops:
  9.9 7.3 %all-to-all-start = ((s32[32,1,258]{2,1,0:T(1,128)}), s32[32,1,258]{2,1,0:T(1,128)S(1)}, u32[]{:S(2)}, u32[]{:S(2)}) async-start(s32[32,1,258]{2,1,0:T(1,128)} %broadcast_in_dim.85), calls=%async_computation | async-start | bytes 98304 | tf_op jit(solution)/shard_map/all_to_all | solution.py:46
  18.8 5.7 all-to-all-done
  24.7 11.4 %gather_fusion.4 = bf16[3072,128]{1,0:T(8,128)(2,1)} fusion(bf16[128,3072]{0,1:T(8,128)(2,1)S(1)} %copy.84, s32[3072]{0:T(1024)S(1)} %broadcast_clamp_fusion.1), kind=kCustom, calls=%fused_computation.4 | custom fusion | bytes 1585152 | tf_op jit(solution)/shard_map/jit(_take)/gather | solution.py:104
  45.9 5.1 copy.105
  54.2 4.3 gather_fusion.1
  58.5 4.5 copy.81
  63.0 4.4 gather_fusion.2
  67.4 4.6 copy.82
  72.2 34.0 %all-to-all-done.1 = bf16[32,4,24,256]{3,2,1,0:T(8,128)(2,1)S(1)} async-done(((bf16[32,4,24,256]{3,2,1,0:T(8,128)(2,1)}), bf16[32,4,24,256]{3,2,1,0:T(8,128)(2,1)S(1)}, u32[]{:S(2)}, u32[]{:S(2)}) %all-to-all-start.1) | async-done | bytes 1572896 | tf_op jit(solution)/shard_map/all_to_all | solution.py:108
  109.7 50.7 %all-gather.12.cloned.1.call-done = bf16[1024,3072]{0,1:T(8,128)(2,1)} async-done(((bf16[128,3072]{0,1:T(8,128)(2,1)}), bf16[1024,3072]{0,1:T(8,128)(2,1)}) %all-gather.12.cloned.1.call-update) | async-done | bytes 6291472 | tf_op jit(solution)/shard_map/all_gather | solution.py:105
  167.9 56.2 %all-gather.6.cloned.1.call-done = bf16[3,3072,256]{1,2,0:T(8,128)(2,1)} async-done(((bf16[3,768,256]{1,2,0:T(8,128)(2,1)}), bf16[3,3072,256]{1,2,0:T(8,128)(2,1)}) %all-gather.6.cloned.1.call-update) | async-done | bytes 4718608 | tf_op jit(solution)/shard_map/all_gather | solution.py:122
  224.1 8.5 %fusion.12 = bf16[3,1024,256]{1,2,0:T(8,128)(2,1)S(1)} fusion(bf16[3,3072,256]{1,2,0:T(8,128)(2,1)} %all-gather.6.cloned.1.call-done, bf16[1024,3072]{0,1:T(8,128)(2,1)} %all-gather.12.cloned.1.call-done), kind=kOutput, calls=%fused_computation.28 | convolution fusion | flops 4832624640 | bytes 12582912 | tf_op jit(solution)/shard_map/sr,mrc->msc/dot_general | solution.py:123
  233.9 8.7 %fusion.22 = (f32[2,1024]{1,0:T(2,128)S(1)}, f32[2,1024,1024]{1,2,0:T(8,128)}) fusion(pred[1024,1024]{0,1:T(8,128)(4,1)S(1)} %fusion.6, bf16[1024,2,128]{0,2,1:T(8,128)(2,1)} %bitcast.102, bf16[1024,2,128]{0,2,1:T(8,128)(2,1)} %bitcast.101), kind=kOutput, calls=%fused_computation.60 | convolution fusion | flops 547357696 | bytes 10493952 | tf_op jit(solution)/shard_map/sub | solution.py:137
  242.5 4.3 fusion.15
  250.7 5.9 %convolution_convert_fusion = bf16[1024,3072]{1,0:T(8,128)(2,1)} fusion(bf16[1024,256]{0,1:T(8,128)(2,1)S(1)} %bitcast.99, bf16[3072,256]{1,0:T(8,128)(2,1)} %all-gather.8.cloned.1.call-done), kind=kOutput, calls=%fused_computation.15 | convolution fusion | flops 1613758464 | bytes 8388608 | tf_op jit(solution)/shard_map/sc,rc->sr/dot_general | solution.py:141
  257.1 119.5 %reduce-scatter.2.cloned.1.call-done = bf16[128,3072]{1,0:T(8,128)(2,1)} async-done(((bf16[1024,3072]{1,0:T(8,128)(2,1)}), bf16[128,3072]{1,0:T(8,128)(2,1)}) %reduce-scatter.2.cloned.1.call-update) | async-done | bytes 786448 | tf_op jit(solution)/shard_map/reduce_scatter | solution.py:155
  378.0 11.5 %gather_fusion.7 = bf16[3072,128]{1,0:T(8,128)(2,1)} fusion(bf16[128,3072]{0,1:T(8,128)(2,1)S(1)} %copy.94, s32[3072]{0:T(1024)S(1)} %broadcast_clamp_fusion), kind=kCustom, calls=%fused_computation.7 | custom fusion | bytes 1585152 | tf_op jit(solution)/shard_map/jit(_take)/gather | solution.py:156
  393.7 4.2 all-to-all-start.3
  397.9 149.0 %all-gather.10.cloned.1.call-done = bf16[1024,3072]{0,1:T(8,128)(2,1)} async-done(((bf16[128,3072]{0,1:T(8,128)(2,1)}), bf16[1024,3072]{0,1:T(8,128)(2,1)}) %all-gather.10.cloned.1.call-update) | async-done | bytes 6291472 | tf_op jit(solution)/shard_map/all_gather | solution.py:162
  546.9 10.7 %fusion.23 = (f32[1024]{0:T(1024)S(1)}, f32[1024,1024]{0,1:T(8,128)S(1)}) fusion(bf16[1024,3072]{0,1:T(8,128)(2,1)} %all-gather.10.cloned.1.call-done, bf16[3072,1024]{1,0:T(8,128)(2,1)} %param.19), kind=kOutput, calls=%fused_computation.61 | convolution fusion | flops 6443498496 | bytes 16781312 | tf_op jit(solution)/shard_map/dot_general | solution.py:163
  559.7 4.7 all-to-all-start.4
  565.6 4.3 gather_fusion.5
  569.9 3.9 copy.91
  573.8 4.3 gather_fusion.6
  (70 shorter events, 45.9 us)
Async XLA Ops:
  9.9 14.6 %all-to-all-start = ((s32[32,1,258]{2,1,0:T(1,128)}), s32[32,1,258]{2,1,0:T(1,128)S(1)}, u32[]{:S(2)}, u32[]{:S(2)}) async-start(s32[32,1,258]{2,1,0:T(1,128)} %broadcast_in_dim.85), calls=%async_computation | async-start | bytes 98304 | tf_op jit(solution)/shard_map/all_to_all | solution.py:46
  17.2 143.2 %all-gather.12.cloned.1.call-start = ((), (), s32[]{:S(2)}) async-start(), calls=%async_computation.10 | async-start | bytes 7077888 | tf_op jit(solution)/shard_map/all_gather | solution.py:105
  24.4 11.8 %copy-start.2 = (s32[32,1,258]{2,1,0:T(1,128)}, s32[32,1,258]{2,1,0:T(1,128)S(1)}, u32[]{:S(2)}) copy-start(s32[32,1,258]{2,1,0:T(1,128)S(1)} %all-to-all-done) | copy-start | bytes 99076
  43.2 63.1 %all-to-all-start.1 = ((bf16[32,4,24,256]{3,2,1,0:T(8,128)(2,1)}), bf16[32,4,24,256]{3,2,1,0:T(8,128)(2,1)S(1)}, u32[]{:S(2)}, u32[]{:S(2)}) async-start(bf16[32,4,24,256]{3,2,1,0:T(8,128)(2,1)} %bitcast.1), calls=%async_computation.1 | async-start | bytes 3145728 | tf_op jit(solution)/shard_map/all_to_all | solution.py:108
  45.9 178.3 %all-gather.6.cloned.1.call-start = ((), (), s32[]{:S(2)}) async-start(), calls=%async_computation.6 | async-start | bytes 5898240 | tf_op jit(solution)/shard_map/all_gather | solution.py:122
  45.9 5.1 copy-start.1
  106.3 1.1 copy-start
  161.9 94.7 %all-to-all-start.2 = ((f32[32,4,24,256]{3,2,1,0:T(8,128)}), f32[32,4,24,256]{3,2,1,0:T(8,128)}, u32[]{:S(2)}, u32[]{:S(2)}) async-start(f32[32,4,24,256]{3,2,1,0:T(8,128)} %bitcast.81), calls=%async_computation.2 | async-start | bytes 6291456 | tf_op jit(solution)/shard_map/all_to_all | solution.py:121
  165.5 85.2 %all-gather.8.cloned.1.call-start = ((), (), s32[]{:S(2)}) async-start(), calls=%async_computation.7 | async-start | bytes 1966080 | tf_op jit(solution)/shard_map/all_gather | solution.py:144
  167.7 208.8 %reduce-scatter.2.cloned.1.call-start = ((), (), s32[]{:S(2)}) async-start(), calls=%async_computation.8 | async-start | bytes 7077888 | tf_op jit(solution)/shard_map/reduce_scatter | solution.py:155
  256.6 290.3 %all-gather.10.cloned.1.call-start = ((), (), s32[]{:S(2)}) async-start(), calls=%async_computation.9 | async-start | bytes 7077888 | tf_op jit(solution)/shard_map/all_gather | solution.py:162
  378.0 13.1 %copy-start.3 = (f32[3072]{0:T(1024)S(1)}, f32[3072]{0:T(1024)}, u32[]{:S(2)}) copy-start(f32[3072]{0:T(1024)} %param.18) | copy-start | bytes 36868
  393.7 166.0 %all-to-all-start.3 = ((f32[32,4,24,256]{3,2,1,0:T(8,128)}), f32[32,4,24,256]{3,2,1,0:T(8,128)}, u32[]{:S(2)}, u32[]{:S(2)}) async-start(f32[32,4,24,256]{3,2,1,0:T(8,128)} %bitcast.80), calls=%async_computation.3 | async-start | bytes 6291456 | tf_op jit(solution)/shard_map/all_to_all | solution.py:154
  559.7 22.3 %all-to-all-start.4 = ((f32[8,3,128]{2,1,0:T(4,128)}), f32[8,3,128]{2,1,0:T(4,128)S(1)}, u32[]{:S(2)}, u32[]{:S(2)}) async-start(f32[8,3,128]{2,1,0:T(4,128)} %maximum_bitcast_fusion), calls=%async_computation.5 | async-start | bytes 32768 | tf_op jit(solution)/shard_map/all_to_all | solution.py:62
Sparse Core Ops, SparseCore 0:
  36.3 124.0 all-gather.11
  162.5 61.5 all-gather.5
  225.7 24.9 all-gather.7
  256.7 119.7 reduce-scatter.1
  393.8 153.0 all-gather.9
where the time goes:
time: 590 us; the launch traced here: 589 us
  waiting for transfers between devices  419 us (71%)
  local copies, waits for them, and re-layouts  85.3 us (14%)
  matrix products  38.1 us (6%)
  starting transfers between devices  22.9 us (4%)
  between operations  15.3 us (3%)
  other arithmetic  8.52 us (1%)
    all_gather x1, waiting for transfers between devices, body(): normed = lax.all_gather(own_normed, ('fsdp', 'mp'), axis=0, tiled=True)  149 us
    reduce_scatter x1, waiting for transfers between devices, body(): lax.psum_scatter(partial_value, ('fsdp', 'mp'), scatter_dimension=0, tile...  119 us
    all_gather x1, waiting for transfers between devices, body(): piece = lax.all_gather(projections, 'dp', axis=1, tiled=True)  56.2 us
    all_gather x1, waiting for transfers between devices, body(): picked_cols = lax.all_gather(own_picked, ('fsdp', 'mp'), axis=0, tiled=True)  50.7 us
    all_to_all x1, waiting for transfers between devices, body(): lax.all_to_all(weights_sent, everyone, split_axis=0, concat_axis=0, tiled...  34 us
    unnamed x14, local copies, waits for them, and re-layouts  12.8 us
    transpose x3, local copies, waits for them, and re-layouts, pack_rows(): chosen.transpose(2, 3, 0, 1, 4)  12.3 us
  transfers between devices with their start and end apart: 10, of which 7 were waited for; matrix products, arithmetic and copies ran while one was open for 17% of the time, Pallas kernels for 0%

commit v1 on v0

--- a/solution.py
+++ b/solution.py
@@ -5,6 +5,18 @@
 from jax.sharding import PartitionSpec as P
 
 HD = 128
+
+
+def ring_product(shard, axis, dim, term):
+    size, index, rows = (lax.axis_size(axis), lax.axis_index(axis), shard.shape[dim])
+    right = [(i, (i + 1) % size) for i in range(size)]
+    held, total = (shard, None)
+    for step in range(size):
+        coming = lax.ppermute(held, axis, right) if step < size - 1 else None
+        absorb = term(held, (index - step) % size * rows)
+        total = absorb if total is None else total + absorb
+        held = coming
+    return total
 
 
 def inverse_of(table):
@@ -119,8 +131,17 @@
             (picked_cols, projections, first_sent)
         )
     first_got = lax.all_to_all(first_sent, everyone, split_axis=0, concat_axis=0, tiled=True)
-    piece = lax.all_gather(projections, "dp", axis=1, tiled=True)
-    projected = jnp.einsum("sr,mrc->msc", picked_cols, piece, preferred_element_type=jnp.float32)
+    projected = ring_product(
+        projections,
+        "dp",
+        1,
+        lambda part, start: jnp.einsum(
+            "sr,mrc->msc",
+            lax.dynamic_slice_in_dim(picked_cols, start, part.shape[1], axis=1),
+            part,
+            preferred_element_type=jnp.float32,
+        ),
+    )
     heads = group_cols // HD
     queries = projected[0].astype(jnp.bfloat16).reshape(seq_len, heads, HD)
     keys_all = projected[1].astype(jnp.bfloat16).reshape(seq_len, heads, HD)

time: 590 us -> 602 us (1.020)
    ppermute x0 -> x3, waiting for transfers between devices: none -> 67.3 us  [ring_product(): coming = lax.ppermute(held, axis, right) if step < size - 1 else None]
    all_gather x1 -> x0, waiting for transfers between devices: 56.2 us -> none  [body(): piece = lax.all_gather(projections, 'dp', axis=1, tiled=True)]
    dot_general x1 -> x4, matrix products: 8.53 us -> 12.5 us  [body(): jnp.einsum('sr,mrc->msc', lax.dynamic_slice_in_dim(picked_cols, start, pa...]
    unnamed x14 -> x16, local copies, waits for them, and re-layouts: 12.8 us -> 13.7 us
  transfers between devices with their start and end apart: 10 -> 12, of which waited for: 7 -> 8; matrix products, arithmetic and copies ran while one was open for 17% -> 17% of each run, Pallas kernels for 0% -> 0%
where the time goes in v1:
time: 602 us; the launch traced here: 601 us
  waiting for transfers between devices  425 us (71%)
  local copies, waits for them, and re-layouts  85 us (14%)
  matrix products  42.1 us (7%)
  starting transfers between devices  22.8 us (4%)
  between operations  16.7 us (3%)
  other arithmetic  9.49 us (2%)
    all_gather x1, waiting for transfers between devices, body(): normed = lax.all_gather(own_normed, ('fsdp', 'mp'), axis=0, tiled=True)  149 us
    reduce_scatter x1, waiting for transfers between devices, body(): lax.psum_scatter(partial_value, ('fsdp', 'mp'), scatter_dimension=0, tile...  119 us
    ppermute x3, waiting for transfers between devices, ring_product(): coming = lax.ppermute(held, axis, right) if step < size - 1 else None  67.3 us
    all_gather x1, waiting for transfers between devices, body(): picked_cols = lax.all_gather(own_picked, ('fsdp', 'mp'), axis=0, tiled=True)  49.4 us
    all_to_all x1, waiting for transfers between devices, body(): lax.all_to_all(weights_sent, everyone, split_axis=0, concat_axis=0, tiled...  33.9 us
    unnamed x16, local copies, waits for them, and re-layouts  13.7 us
    dot_general x4, matrix products, body(): jnp.einsum('sr,mrc->msc', lax.dynamic_slice_in_dim(picked_cols, start, pa...  12.5 us
    transpose x3, local copies, waits for them, and re-layouts, pack_rows(): chosen.transpose(2, 3, 0, 1, 4)  12.3 us
  transfers between devices with their start and end apart: 12, of which 8 were waited for; matrix products, arithmetic and copies ran while one was open for 17% of the time, Pallas kernels for 0%

profile of v1, /device:TPU:0, one launch (start us, length us, event | category | flops | bytes accessed | tf_op | source)
XLA Modules:
  0.0 600.8 jit_solution(17647871988592214942)
XLA Ops:
  10.7 7.3 %all-to-all-start = ((s32[32,1,258]{2,1,0:T(1,128)}), s32[32,1,258]{2,1,0:T(1,128)S(1)}, u32[]{:S(2)}, u32[]{:S(2)}) async-start(s32[32,1,258]{2,1,0:T(1,128)} %broadcast_in_dim.85), calls=%async_computation | async-start | bytes 98304 | tf_op jit(solution)/shard_map/all_to_all | solution.py:58
  19.6 5.7 all-to-all-done
  25.9 9.1 %gather_fusion.4 = bf16[3072,128]{1,0:T(8,128)(2,1)S(1)} fusion(bf16[128,3072]{0,1:T(8,128)(2,1)S(1)} %copy.88, s32[3072]{0:T(1024)S(1)} %broadcast_clamp_fusion.1), kind=kCustom, calls=%fused_computation.4 | custom fusion | bytes 1585152 | tf_op jit(solution)/shard_map/jit(_take)/gather | solution.py:116
  45.9 5.1 copy.109
  54.2 4.3 gather_fusion.1
  58.5 4.5 copy.85
  63.1 4.3 gather_fusion.2
  67.4 4.6 copy.86
  72.2 33.9 %all-to-all-done.1 = bf16[32,4,24,256]{3,2,1,0:T(8,128)(2,1)S(1)} async-done(((bf16[32,4,24,256]{3,2,1,0:T(8,128)(2,1)}), bf16[32,4,24,256]{3,2,1,0:T(8,128)(2,1)S(1)}, u32[]{:S(2)}, u32[]{:S(2)}) %all-to-all-start.1) | async-done | bytes 1572896 | tf_op jit(solution)/shard_map/all_to_all | solution.py:120
  109.6 49.4 %all-gather.9.cloned.1.call-done = bf16[1024,3072]{1,0:T(8,128)(2,1)} async-done(((bf16[128,3072]{1,0:T(8,128)(2,1)}), bf16[1024,3072]{1,0:T(8,128)(2,1)}) %all-gather.9.cloned.1.call-update) | async-done | bytes 6291472 | tf_op jit(solution)/shard_map/all_gather | solution.py:117
  164.1 28.9 %collective-permute-done = bf16[3,768,256]{1,2,0:T(8,128)(2,1)} collective-permute-done((bf16[3,768,256]{1,2,0:T(8,128)(2,1)}, bf16[3,768,256]{1,2,0:T(8,128)(2,1)}, u32[]{:S(2)}, u32[]{:S(2)}) %collective-permute-start) | collective-permute-done | bytes 1179680 | tf_op jit(solution)/shard_map/ppermute | solution.py:15
  193.8 23.5 %collective-permute-done.1 = bf16[3,768,256]{1,2,0:T(8,128)(2,1)} collective-permute-done((bf16[3,768,256]{1,2,0:T(8,128)(2,1)}, bf16[3,768,256]{1,2,0:T(8,128)(2,1)}, u32[]{:S(2)}, u32[]{:S(2)}) %collective-permute-start.1) | collective-permute-done | bytes 1179680 | tf_op jit(solution)/shard_map/ppermute | solution.py:15
  229.2 14.8 %collective-permute-done.2 = bf16[3,768,256]{1,2,0:T(8,128)(2,1)} collective-permute-done((bf16[3,768,256]{1,2,0:T(8,128)(2,1)}, bf16[3,768,256]{1,2,0:T(8,128)(2,1)}, u32[]{:S(2)}, u32[]{:S(2)}) %collective-permute-start.2) | collective-permute-done | bytes 1179680 | tf_op jit(solution)/shard_map/ppermute | solution.py:15
  249.1 8.7 %fusion.32 = (f32[2,1024]{1,0:T(2,128)S(1)}, f32[2,1024,1024]{1,2,0:T(8,128)}) fusion(pred[1024,1024]{0,1:T(8,128)(4,1)S(1)} %copy-done.2, bf16[1024,2,128]{0,2,1:T(8,128)(2,1)} %bitcast.113, bf16[1024,2,128]{0,2,1:T(8,128)(2,1)} %bitcast.112), kind=kOutput, calls=%fused_computation.73 | convolution fusion | flops 547357696 | bytes 10493952 | tf_op jit(solution)/shard_map/sub | solution.py:158
  257.7 4.3 fusion.21
  262.1 5.9 convolution_convert_fusion
  268.7 119.0 %reduce-scatter.2.cloned.1.call-done = bf16[128,3072]{1,0:T(8,128)(2,1)} async-done(((bf16[1024,3072]{1,0:T(8,128)(2,1)}), bf16[128,3072]{1,0:T(8,128)(2,1)}) %reduce-scatter.2.cloned.1.call-update) | async-done | bytes 786448 | tf_op jit(solution)/shard_map/reduce_scatter | solution.py:176
  389.2 11.5 %gather_fusion.7 = bf16[3072,128]{1,0:T(8,128)(2,1)} fusion(bf16[128,3072]{0,1:T(8,128)(2,1)S(1)} %copy.99, s32[3072]{0:T(1024)S(1)} %broadcast_clamp_fusion), kind=kCustom, calls=%fused_computation.7 | custom fusion | bytes 1585152 | tf_op jit(solution)/shard_map/jit(_take)/gather | solution.py:177
  404.9 4.0 all-to-all-start.3
  408.9 149.2 %all-gather.7.cloned.1.call-done = bf16[1024,3072]{0,1:T(8,128)(2,1)} async-done(((bf16[128,3072]{0,1:T(8,128)(2,1)}), bf16[1024,3072]{0,1:T(8,128)(2,1)}) %all-gather.7.cloned.1.call-update) | async-done | bytes 6291472 | tf_op jit(solution)/shard_map/all_gather | solution.py:183
  558.1 10.7 %fusion.33 = (f32[1024]{0:T(1024)S(1)}, f32[1024,1024]{0,1:T(8,128)S(1)}) fusion(bf16[1024,3072]{0,1:T(8,128)(2,1)} %all-gather.7.cloned.1.call-done, bf16[3072,1024]{1,0:T(8,128)(2,1)} %param.19), kind=kOutput, calls=%fused_computation.74 | convolution fusion | flops 6443498496 | bytes 16781312 | tf_op jit(solution)/shard_map/dot_general | solution.py:184
  570.8 4.7 all-to-all-start.4
  576.8 4.3 gather_fusion.5
  584.9 4.3 gather_fusion.6
  (79 shorter events, 61.7 us)
Async XLA Ops:
  10.7 14.6 %all-to-all-start = ((s32[32,1,258]{2,1,0:T(1,128)}), s32[32,1,258]{2,1,0:T(1,128)S(1)}, u32[]{:S(2)}, u32[]{:S(2)}) async-start(s32[32,1,258]{2,1,0:T(1,128)} %broadcast_in_dim.85), calls=%async_computation | async-start | bytes 98304 | tf_op jit(solution)/shard_map/all_to_all | solution.py:58
  18.0 141.0 %all-gather.9.cloned.1.call-start = ((), (), s32[]{:S(2)}) async-start(), calls=%async_computation.9 | async-start | bytes 7077888 | tf_op jit(solution)/shard_map/all_gather | solution.py:117
  25.3 0.6 copy-start.3
  43.2 63.0 %all-to-all-start.1 = ((bf16[32,4,24,256]{3,2,1,0:T(8,128)(2,1)}), bf16[32,4,24,256]{3,2,1,0:T(8,128)(2,1)S(1)}, u32[]{:S(2)}, u32[]{:S(2)}) async-start(bf16[32,4,24,256]{3,2,1,0:T(8,128)(2,1)} %bitcast.1), calls=%async_computation.1 | async-start | bytes 3145728 | tf_op jit(solution)/shard_map/all_to_all | solution.py:120
  45.9 5.1 copy-start.1
  106.2 1.1 copy-start
  160.5 32.5 %collective-permute-start = (bf16[3,768,256]{1,2,0:T(8,128)(2,1)}, bf16[3,768,256]{1,2,0:T(8,128)(2,1)}, u32[]{:S(2)}, u32[]{:S(2)}) collective-permute-start(bf16[3,768,256]{1,2,0:T(8,128)(2,1)} %copy.92), channel_id=1, source_target_pairs={{0,8},{8,16},{16,24},{24,0},{1,9},{9,17},{17,25},{25,1},{2,10},{10... | collective-permute-start | bytes 3538952 | tf_op jit(solution)/shard_map/ppermute | solution.py:15
  160.5 107.5 %all-to-all-start.2 = ((f32[32,4,24,256]{3,2,1,0:T(8,128)}), f32[32,4,24,256]{3,2,1,0:T(8,128)}, u32[]{:S(2)}, u32[]{:S(2)}) async-start(f32[32,4,24,256]{3,2,1,0:T(8,128)} %bitcast.91), calls=%async_computation.2 | async-start | bytes 6291456 | tf_op jit(solution)/shard_map/all_to_all | solution.py:133
  164.1 98.0 %all-gather.5.cloned.1.call-start = ((), (), s32[]{:S(2)}) async-start(), calls=%async_computation.6 | async-start | bytes 1966080 | tf_op jit(solution)/shard_map/all_gather | solution.py:165
  193.1 24.3 %collective-permute-start.1 = (bf16[3,768,256]{1,2,0:T(8,128)(2,1)}, bf16[3,768,256]{1,2,0:T(8,128)(2,1)}, u32[]{:S(2)}, u32[]{:S(2)}) collective-permute-start(bf16[3,768,256]{1,2,0:T(8,128)(2,1)} %collective-permute-done), channel_id=1, source_target_pairs={{0,8},{8,16},{16,24},{24,0},{1,9},{9,17},{17,25},{25,1},{2,10},{10... | collective-permute-start | bytes 3538952 | tf_op jit(solution)/shard_map/ppermute | solution.py:15
  217.3 26.7 %collective-permute-start.2 = (bf16[3,768,256]{1,2,0:T(8,128)(2,1)}, bf16[3,768,256]{1,2,0:T(8,128)(2,1)}, u32[]{:S(2)}, u32[]{:S(2)}) collective-permute-start(bf16[3,768,256]{1,2,0:T(8,128)(2,1)} %collective-permute-done.1), channel_id=1, source_target_pairs={{0,8},{8,16},{16,24},{24,0},{1,9},{9,17},{17,25},{25,1},{2,10},{10... | collective-permute-start | bytes 3538952 | tf_op jit(solution)/shard_map/ppermute | solution.py:15
  219.7 168.0 %reduce-scatter.2.cloned.1.call-start = ((), (), s32[]{:S(2)}) async-start(), calls=%async_computation.7 | async-start | bytes 7077888 | tf_op jit(solution)/shard_map/reduce_scatter | solution.py:176
  247.3 1.8 copy-start.2
  268.0 290.1 %all-gather.7.cloned.1.call-start = ((), (), s32[]{:S(2)}) async-start(), calls=%async_computation.8 | async-start | bytes 7077888 | tf_op jit(solution)/shard_map/all_gather | solution.py:183
  389.2 13.1 %copy-start.4 = (f32[3072]{0:T(1024)S(1)}, f32[3072]{0:T(1024)}, u32[]{:S(2)}) copy-start(f32[3072]{0:T(1024)} %param.18) | copy-start | bytes 36868
  404.9 166.0 %all-to-all-start.3 = ((f32[32,4,24,256]{3,2,1,0:T(8,128)}), f32[32,4,24,256]{3,2,1,0:T(8,128)}, u32[]{:S(2)}, u32[]{:S(2)}) async-start(f32[32,4,24,256]{3,2,1,0:T(8,128)} %bitcast.90), calls=%async_computation.3 | async-start | bytes 6291456 | tf_op jit(solution)/shard_map/all_to_all | solution.py:175
  570.8 22.3 %all-to-all-start.4 = ((f32[8,3,128]{2,1,0:T(4,128)}), f32[8,3,128]{2,1,0:T(4,128)S(1)}, u32[]{:S(2)}, u32[]{:S(2)}) async-start(f32[8,3,128]{2,1,0:T(4,128)} %maximum_bitcast_fusion), calls=%async_computation.5 | async-start | bytes 32768 | tf_op jit(solution)/shard_map/all_to_all | solution.py:74
Sparse Core Ops, SparseCore 0:
  36.4 122.5 all-gather.8
  268.1 119.5 reduce-scatter.1
  405.0 153.0 all-gather.6
Sparse Core Ops, SparseCore 1:
  219.8 28.1 all-gather.4
